TPU v7x, 8 devices: a whole 2x2x1 slice. The times are simulated.
8 devices in a mesh: row: 2 (over z, y), col: 4 (over x, core).
Axes of the slice: x: 2, y: 2, z: 1, core: 2. Of those that a mesh axis runs over, the one named last changes fastest.
Arguments:
- v_panels: float32 [6144, 6144], P('row', 'col')
- t_factors: float32 [96, 64, 64], P('col')
- z_vectors: float32 [6144, 2048], P(None, ('col', 'row'))
Outputs:
- output: float32 [6144, 2048], P('row', 'col')
All inputs are finite; a program needn't handle non-finite values.
Results may differ from a plain program's by a relative error of at most 0.001.
Values sent between devices are 32-bit elements.
A program may use at most 1 GiB of HBM per device.

v0:
```python
import jax
import jax.numpy as jnp
from jax import lax
from jax.sharding import PartitionSpec as P

FULL_PRECISION = lax.Precision.HIGHEST


def solution(mesh):
    def local_program(v_local, t_local, z_local):
        x_start = lax.all_to_all(z_local, "row", 0, 1, tiled=True)
        v_rows = lax.all_gather(v_local, "col", axis=1, tiled=True)
        t_all = lax.all_gather(t_local, "col", axis=0, tiled=True)
        panel_count = t_all.shape[0]
        width = t_all.shape[1]

        def apply_panel(step, x_cur):
            panel_idx = panel_count - 1 - step
            v_pan = lax.dynamic_slice_in_dim(v_rows, panel_idx * width, width, axis=1)
            t_pan = lax.dynamic_index_in_dim(t_all, panel_idx, axis=0, keepdims=False)
            w_part = lax.dot_general(v_pan, x_cur, (((0,), (0,)), ((), ())), precision=FULL_PRECISION, preferred_element_type=jnp.float32)
            w_full = lax.psum(w_part, "row")
            y_mat = jnp.dot(t_pan, w_full, precision=FULL_PRECISION, preferred_element_type=jnp.float32)
            return x_cur - jnp.dot(v_pan, y_mat, precision=FULL_PRECISION, preferred_element_type=jnp.float32)

        return lax.fori_loop(0, panel_count, apply_panel, x_start)

    return jax.shard_map(local_program, mesh=mesh, in_specs=(P("row", "col"), P("col", None, None), P(None, ("col", "row"))), out_specs=P("row", "col"), check_vma=False)
```

profile of v0, /device:TPU:3, one launch (start us, length us, event | category | flops | bytes accessed | tf_op | source)
XLA Modules:
  0.0 3790.1 jit_solution(11160478700792549800)
XLA Ops:
  14.3 69.3 %all-to-all-done = f32[2,3072,256]{2,1,0:T(8,128)} async-done(((f32[2,3072,256]{2,1,0:T(8,128)}), f32[2,3072,256]{2,1,0:T(8,128)}, u32[]{:S(2)}, u32[]{:S(2)}) %all-to-all-start) | async-done | bytes 6291488 | tf_op jit(solution)/shard_map/all_to_all | solution.py:11
  97.1 378.0 %all-gather.3.cloned.1.call-done = f32[3072,6144]{1,0:T(8,128)} async-done(((f32[3072,1536]{1,0:T(8,128)}), f32[3072,6144]{1,0:T(8,128)}) %all-gather.3.cloned.1.call-update) | async-done | bytes 75497488 | tf_op jit(solution)/shard_map/all_gather | solution.py:12
  475.2 3308.4 %while.15 = (s32[]{:T(128)}, f32[3072,512]{1,0:T(8,128)}, f32[3072,6144]{1,0:T(8,128)}, f32[96,64,64]{2,1,0:T(8,128)}, s32[]{:T(128)}, /*index=5*/s32[]{:T(128)}, s32[]{:T(128)}, s32[]{:T(128)}, s32[]{:T(128)}, s32[]{:T(128)}) while((s32[]{:T(128)}, f32[3072,512]{1,0:T(8,128)}, f32[3072,6144]{1,0:T(8,128)}, f32[96,64,64]{2,1,0:T(8,128)}, ...), condition=%wide.region_2.3_spmd, body=%wide.region_0.2_spmd.sunk | while | flops 2442690560 | bytes 23363836 | solution.py:26
  483.0 16.3 all-reduce.2.cloned.1.call-done
  517.6 16.1 all-reduce.2.cloned.1.call-done
  552.1 16.1 all-reduce.2.cloned.1.call-done
  621.1 16.1 all-reduce.2.cloned.1.call-done
  655.5 16.1 all-reduce.2.cloned.1.call-done
  690.0 16.1 all-reduce.2.cloned.1.call-done
  758.9 16.1 all-reduce.2.cloned.1.call-done
  793.3 16.1 all-reduce.2.cloned.1.call-done
  931.1 16.1 all-reduce.2.cloned.1.call-done
  965.6 16.1 all-reduce.2.cloned.1.call-done
  1069.1 16.1 all-reduce.2.cloned.1.call-done
  1103.6 16.1 all-reduce.2.cloned.1.call-done
  1172.5 16.1 all-reduce.2.cloned.1.call-done
  1206.9 16.1 all-reduce.2.cloned.1.call-done
  1275.8 16.1 all-reduce.2.cloned.1.call-done
  1310.3 16.1 all-reduce.2.cloned.1.call-done
  1379.2 16.1 all-reduce.2.cloned.1.call-done
  1482.7 16.1 all-reduce.2.cloned.1.call-done
  1517.1 16.1 all-reduce.2.cloned.1.call-done
  1551.6 16.1 all-reduce.2.cloned.1.call-done
  1586.0 16.1 all-reduce.2.cloned.1.call-done
  (563 shorter events, 2988.1 us)
Async XLA Ops:
  6.5 90.6 %all-gather.5.cloned.1.call-start = ((), (), s32[]{:S(2)}) async-start(), calls=%async_computation.2 | async-start | bytes 3932160 | tf_op jit(solution)/shard_map/all_gather | solution.py:13
  7.3 467.9 %all-gather.3.cloned.1.call-start = ((), (), s32[]{:S(2)}) async-start(), calls=%async_computation.1 | async-start | bytes 94371840 | tf_op jit(solution)/shard_map/all_gather | solution.py:12
  8.0 75.6 %all-to-all-start = ((f32[2,3072,256]{2,1,0:T(8,128)}), f32[2,3072,256]{2,1,0:T(8,128)}, u32[]{:S(2)}, u32[]{:S(2)}) async-start(f32[2,3072,256]{2,1,0:T(8,128)} %bitcast.19), calls=%async_computation | async-start | bytes 12582912 | tf_op jit(solution)/shard_map/all_to_all | solution.py:11
  475.2 24.1 all-reduce.2.cloned.1.call-start
  509.9 23.9 all-reduce.2.cloned.1.call-start
  544.3 23.9 all-reduce.2.cloned.1.call-start
  578.8 23.9 all-reduce.2.cloned.1.call-start
  613.3 23.9 all-reduce.2.cloned.1.call-start
  647.7 23.9 all-reduce.2.cloned.1.call-start
  682.2 23.9 all-reduce.2.cloned.1.call-start
  751.1 23.9 all-reduce.2.cloned.1.call-start
  785.5 23.9 all-reduce.2.cloned.1.call-start
  888.9 23.9 all-reduce.2.cloned.1.call-start
  923.4 23.9 all-reduce.2.cloned.1.call-start
  957.8 23.9 all-reduce.2.cloned.1.call-start
  1061.3 23.9 all-reduce.2.cloned.1.call-start
  1095.8 23.9 all-reduce.2.cloned.1.call-start
  1164.7 23.9 all-reduce.2.cloned.1.call-start
  1199.1 23.9 all-reduce.2.cloned.1.call-start
  1268.0 23.9 all-reduce.2.cloned.1.call-start
  1302.5 23.9 all-reduce.2.cloned.1.call-start
  1371.4 23.9 all-reduce.2.cloned.1.call-start
  1578.2 23.9 all-reduce.2.cloned.1.call-start
  1612.7 23.9 all-reduce.2.cloned.1.call-start
  (75 other events, 1792.1 us)
Sparse Core Ops, SparseCore 0:
  8.9 25.9 all-gather.4
  36.4 438.7 all-gather.2
  483.1 16.1 all-reduce.1
  517.8 15.9 all-reduce.1
  552.2 15.9 all-reduce.1
  621.2 15.9 all-reduce.1
  655.6 15.9 all-reduce.1
  690.1 15.9 all-reduce.1
  724.5 15.9 all-reduce.1
  759.0 15.9 all-reduce.1
  793.4 15.9 all-reduce.1
  827.9 15.9 all-reduce.1
  896.8 15.9 all-reduce.1
  931.3 15.9 all-reduce.1
  965.7 15.9 all-reduce.1
  1069.2 15.9 all-reduce.1
  1103.7 15.9 all-reduce.1
  1138.1 15.9 all-reduce.1
  1172.6 15.9 all-reduce.1
  1207.0 15.9 all-reduce.1
  1241.5 15.9 all-reduce.1
  1275.9 15.9 all-reduce.1
  1310.4 15.9 all-reduce.1
  1344.8 15.9 all-reduce.1
  (74 shorter events, 1177.5 us)
where the time goes:
time: 3800 us; the launch traced here: 3790 us
  waiting for transfers between devices  2000 us (53%)
  matrix products  1760 us (46%)
    psum x96, waiting for transfers between devices, apply_panel(): w_full = lax.psum(w_part, 'row')  1550 us
    dot_general x96, matrix products, apply_panel(): jnp.dot(v_pan, y_mat, precision=FULL_PRECISION, preferred_element_type=jn...  899 us
    dot_general x96, matrix products, apply_panel(): lax.dot_general(v_pan, x_cur, (((0,), (0,)), ((), ())), precision=FULL_PR...  743 us
    all_gather x1, waiting for transfers between devices, local_program(): v_rows = lax.all_gather(v_local, 'col', axis=1, tiled=True)  378 us
    dot_general x96, matrix products, apply_panel(): jnp.dot(t_pan, w_full, precision=FULL_PRECISION, preferred_element_type=j...  114 us
  transfers between devices with their start and end apart: 99, of which 98 were waited for; matrix products, arithmetic and copies ran while one was open for 0% of the time, Pallas kernels for 0%

commit v1 on v0

v1 whole, which is shorter than its diff:
```python
import jax
import jax.numpy as jnp
from jax import lax
from jax.experimental import pallas as pl
from jax.experimental.pallas import tpu as pltpu
from jax.sharding import PartitionSpec as P

FULL = lax.Precision.HIGHEST
MESH = pl.DeviceIdType.MESH
NB = 256
TR = 512


def mm(a, b):
    return lax.dot_general(a, b, (((1,), (0,)), ((), ())), precision=FULL, preferred_element_type=jnp.float32)


def mtm(a, b):
    return lax.dot_general(a, b, (((0,), (0,)), ((), ())), precision=FULL, preferred_element_type=jnp.float32)


def kernel(
    v_ref, t_ref, z_ref, out_ref, vall,
    x, vs, tb, gown, grecv, ts, ws, wr, ys,
    far_s, far_r, sib_s, sib_r, dia_s, dia_r, t_s, t_r, w_s, w_r, z_s, z_r, g_s, g_r, loc, ld,
):
    r = lax.axis_index("row")
    c = lax.axis_index("col")
    rows = v_ref.shape[0]
    slots = v_ref.shape[1] // NB
    tiles = rows // TR
    per_row = rows // NB
    sib = c + 1 - 2 * (c % 2)
    far = (c + 2) % 4
    other = 1 - r

    barrier = pltpu.get_barrier_semaphore()
    for dst in ((r, sib), (r, far), (other, c)):
        pl.semaphore_signal(barrier, inc=1, device_id=dst, device_id_type=MESH)
    pl.semaphore_wait(barrier, 3)

    def first_tile(j):
        return lax.min(lax.max(j - per_row * r, 0) * NB // TR, tiles)

    def tile(k):
        return pl.ds(pl.multiple_of(k * TR, TR), TR)

    def each_tile(j, fn):
        def body(k, carry):
            fn(k)
            return carry

        lax.fori_loop(first_tile(j), tiles, body, 0)

    def own_tile(s, k):
        return v_ref.at[tile(k), pl.ds(pl.multiple_of(s * NB, NB), NB)]

    def remote(src, dst, ssem, rsem, to):
        return pltpu.make_async_remote_copy(src_ref=src, dst_ref=dst, send_sem=ssem, recv_sem=rsem, device_id=to, device_id_type=MESH)

    def own_copy(s, k, ssem, rsem, to):
        return remote(own_tile(s, k), vall.at[c * slots + s, tile(k)], ssem.at[s, k], rsem.at[s, k], (r, to))

    def got_copy(j, s, k, ssem, rsem, to):
        return remote(vall.at[j, tile(k)], vall.at[j, tile(k)], ssem.at[s, k], rsem.at[s, k], (r, to))

    def send_far(s):
        each_tile(c * slots + s, lambda k: own_copy(s, k, far_s, far_r, far).start())

    def loop_down(hi, n, fn):
        def body(i, carry):
            fn(hi - i)
            return carry

        lax.fori_loop(0, n, body, 0)

    zc = remote(z_ref.at[pl.ds(pl.multiple_of(other * rows, rows), rows)], x.at[r], z_s, z_r, (other, c))
    zc.start()
    zl = pltpu.make_async_copy(z_ref.at[pl.ds(pl.multiple_of(r * rows, rows), rows)], x.at[r], loc.at[0])
    zl.start()
    tl = pltpu.make_async_copy(t_ref, ts, loc.at[1])
    tl.start()

    odd = c % 2
    even = 1 - odd

    @pl.when(odd == 1)
    def _():
        loop_down(slots - 1, 3, send_far)

    loop_down(slots - 1, slots, lambda s: each_tile(c * slots + s, lambda k: own_copy(s, k, sib_s, sib_r, sib).start()))

    def gram(s):
        j = c * slots + s
        each_tile(j, lambda k: pltpu.make_async_copy(own_tile(s, k), vs.at[0, tile(k)], ld.at[k]).start())
        gown[s] = jnp.zeros((NB, NB), jnp.float32)

        def add(k):
            pltpu.make_async_copy(own_tile(s, k), vs.at[0, tile(k)], ld.at[k]).wait()
            v_t = vs[0, tile(k), :]
            gown[s] = gown[s] + mtm(v_t, v_t)

        each_tile(j, add)

    loop_down(slots - 1, slots, gram)
    tl.wait()

    def merge(s):
        j = c * slots + s
        g = gown[s]
        tb[j] = jnp.zeros((NB, NB), jnp.float32)
        for i in range(2):
            t_a, t_b = ts[4 * s + 2 * i], ts[4 * s + 2 * i + 1]
            o = 128 * i
            tb[j, o : o + 64, o : o + 64] = t_a
            tb[j, o + 64 : o + 128, o + 64 : o + 128] = t_b
            tb[j, o : o + 64, o + 64 : o + 128] = -mm(mm(t_a, g[o : o + 64, o + 64 : o + 128]), t_b)
        tb[j, 0:128, 128:256] = -mm(mm(tb[j, 0:128, 0:128], g[0:128, 128:256]), tb[j, 128:256, 128:256])

    def t_copy(q, i, to):
        part = tb.at[pl.ds(q * slots, slots)]
        return remote(part, part, t_s.at[i], t_r.at[i], (r, to))

    def factors():
        loop_down(slots - 1, slots, merge)
        t_copy(c, 0, sib).start()
        t_copy(c, 1, far).start()

    gc = remote(gown, grecv, g_s, g_r, (other, c))

    @pl.when(c < 2)
    def _():
        gc.start()

    @pl.when((c >= 2) & (r == 1))
    def _():
        factors()

    def rest_far():
        @pl.when(odd == 1)
        def _():
            loop_down(slots - 4, slots - 3, send_far)

        @pl.when(odd == 0)
        def _():
            loop_down(slots - 1, slots, send_far)

    @pl.when(c >= 2)
    def _():
        rest_far()

    def t_get(q):
        @pl.when(q == sib)
        def _():
            t_copy(q, 0, sib).wait_recv()

        @pl.when(q == far)
        def _():
            t_copy(q, 1, far).wait_recv()
            t_copy(q, 2, sib).start()

        @pl.when((q + 2) % 4 == sib)
        def _():
            t_copy(q, 2, sib).wait_recv()

    def acquire(j):
        q, s = j // slots, j % slots
        b = j % 2

        @pl.when(q == sib)
        def _():
            each_tile(j, lambda k: got_copy(j, s, k, sib_s, sib_r, sib).wait_recv())

        @pl.when(q == far)
        def _():
            def pass_on(k):
                got_copy(j, s, k, far_s, far_r, far).wait_recv()
                got_copy(j, s, k, dia_s, dia_r, sib).start()

            each_tile(j, pass_on)

        @pl.when((q + 2) % 4 == sib)
        def _():
            each_tile(j, lambda k: got_copy(j, s, k, dia_s, dia_r, sib).wait_recv())

        @pl.when(q == c)
        def _():
            each_tile(j, lambda k: pltpu.make_async_copy(own_tile(s, k), vs.at[b, tile(k)], ld.at[k]).start())

        @pl.when(q != c)
        def _():
            each_tile(j, lambda k: pltpu.make_async_copy(vall.at[j, tile(k)], vs.at[b, tile(k)], ld.at[k]).start())

        each_tile(j, lambda k: pltpu.make_async_copy(vall.at[j, tile(k)], vs.at[b, tile(k)], ld.at[k]).wait())

    def project(j, p):
        ws[p] = jnp.zeros((NB, NB), jnp.float32)

        def add(k):
            ws[p] = ws[p] + mtm(vs[j % 2, tile(k), :], x[p, tile(k), :])

        each_tile(j, add)

    def update(j, p):
        def sub(k):
            x[p, tile(k), :] = x[p, tile(k), :] - mm(vs[j % 2, tile(k), :], ys[p])

        each_tile(j, sub)

    zl.wait()
    zc.wait()

    def lower(j):
        acquire(j)
        for p in range(2):
            project(j, p)
            ys[p] = mm(tb[j], ws[p])
            update(j, p)

    @pl.when(r == 1)
    def _():
        t_get(3)
        loop_down(4 * slots - 1, slots, lower)

    @pl.when(c < 2)
    def _():
        gc.wait()

        def add(s):
            gown[s] = gown[s] + grecv[s]

        loop_down(slots - 1, slots, add)
        factors()

        @pl.when(odd == 1)
        def _():
            loop_down(slots - 4, slots - 3, send_far)

    @pl.when(r == 1)
    def _():
        t_get(2)
        loop_down(3 * slots - 1, slots, lower)

    @pl.when(c == 0)
    def _():
        loop_down(slots - 1, slots, send_far)

    def w_copy(j, p):
        return remote(ws.at[p], wr.at[p, j % 2], w_s.at[p, j % 2], w_r.at[p, j % 2], (other, c))

    def finish(j, p):
        w_copy(j, p).wait()
        ys[p] = mm(tb[j], ws[p] + wr[p, j % 2])
        update(j, p)

    def both(j):
        acquire(j)
        project(j, 0)
        w_copy(j, 0).start()

        @pl.when(j < 2 * slots - 1)
        def _():
            finish(j + 1, 1)

        project(j, 1)
        w_copy(j, 1).start()
        finish(j, 0)

    t_get(1)
    t_get(0)
    loop_down(2 * slots - 1, 2 * slots, both)
    outs = [pltpu.make_async_copy(x.at[p], out_ref.at[:, pl.ds(p * NB, NB)], loc.at[p]) for p in range(2)]
    outs[0].start()
    finish(0, 1)
    outs[1].start()

    def sent(s):
        j = c * slots + s
        each_tile(j, lambda k: own_copy(s, k, far_s, far_r, far).wait_send())
        each_tile(j, lambda k: own_copy(s, k, sib_s, sib_r, sib).wait_send())
        each_tile(far * slots + s, lambda k: got_copy(far * slots + s, s, k, dia_s, dia_r, sib).wait_send())

    loop_down(slots - 1, slots, sent)

    @pl.when((r == 1) | (c < 2))
    def _():
        t_copy(c, 0, sib).wait_send()
        t_copy(c, 1, far).wait_send()

    @pl.when((r == 1) | (far < 2))
    def _():
        t_copy(far, 2, sib).wait_send()

    for o in outs:
        o.wait()


def solution(mesh):
    def local_program(v, t, z):
        rows, width = v.shape
        slots = width // NB
        f32 = jnp.float32
        any_spec = pl.BlockSpec(memory_space=pl.ANY)
        dma = pltpu.SemaphoreType.DMA
        out, _ = pl.pallas_call(
            kernel,
            out_shape=[jax.ShapeDtypeStruct((rows, 2 * NB), f32), jax.ShapeDtypeStruct((4 * slots, rows, NB), f32)],
            in_specs=[any_spec] * 3,
            out_specs=[any_spec] * 2,
            scratch_shapes=[
                pltpu.VMEM((2, rows, NB), f32),
                pltpu.VMEM((2, rows, NB), f32),
                pltpu.VMEM((4 * slots, NB, NB), f32),
                pltpu.VMEM((slots, NB, NB), f32),
                pltpu.VMEM((slots, NB, NB), f32),
                pltpu.VMEM(t.shape, f32),
                pltpu.VMEM((2, NB, NB), f32),
                pltpu.VMEM((2, 2, NB, NB), f32),
                pltpu.VMEM((2, NB, NB), f32),
                *[dma((slots, rows // TR))] * 6,
                dma((3,)), dma((3,)), dma((2, 2)), dma((2, 2)),
                dma, dma, dma, dma, dma((2,)), dma((rows // TR,)),
            ],
            compiler_params=pltpu.CompilerParams(collective_id=0, has_side_effects=True, vmem_limit_bytes=60 * 1024 * 1024),
        )(v, t, z)
        return out

    return jax.shard_map(local_program, mesh=mesh, in_specs=(P("row", "col"), P("col", None, None), P(None, ("col", "row"))), out_specs=P("row", "col"), check_vma=False)
```

time: 3800 us -> 533 us (0.14)
  waiting for transfers between devices: 2000 us -> 0 us
  matrix products: 1760 us -> 0 us
  Pallas kernels: 0 us -> 526 us
    dot_general x288 -> x0, matrix products: 1760 us -> none  [the longest x96 899 us: apply_panel(): jnp.dot(v_pan, y_mat, precision=FULL_PRECISION, preferred_element_type=jn...]
    psum x96 -> x0, waiting for transfers between devices: 1550 us -> none  [apply_panel(): w_full = lax.psum(w_part, 'row')]
    pallas_call x0 -> x1, Pallas kernels: none -> 526 us  [local_program(): pl.pallas_call(kernel, out_shape=[jax.ShapeDtypeStruct((rows, 2 * NB), f3...]
    all_gather x2 -> x0, waiting for transfers between devices: 378 us -> none  [the longest x1 378 us: local_program(): v_rows = lax.all_gather(v_local, 'col', axis=1, tiled=True)]
    all_to_all x1 -> x0, waiting for transfers between devices: 69.3 us -> none  [local_program(): x_start = lax.all_to_all(z_local, 'row', 0, 1, tiled=True)]
  transfers between devices with their start and end apart: 99 -> 0, of which waited for: 98 -> 0; matrix products, arithmetic and copies ran while one was open for 0% -> 0% of each run, Pallas kernels for 0% -> 0%
where the time goes in v1:
time: 533 us; the launch traced here: 532 us
  Pallas kernels  526 us (99%)
  local copies, waits for them, and re-layouts  6.2 us (1%)
    pallas_call x1, Pallas kernels, local_program(): pl.pallas_call(kernel, out_shape=[jax.ShapeDtypeStruct((rows, 2 * NB), f3...  526 us

profile of v1, /device:TPU:3, one launch (start us, length us, event | category | flops | bytes accessed | tf_op | source)
XLA Modules:
  0.0 532.5 jit_solution(7139754373212010029)
XLA Ops:
  0.0 526.2 %shard_map.37 = (f32[3072,512]{1,0:T(8,128)}, f32[24,3072,256]{2,1,0:T(8,128)}) custom-call(f32[3072,1536]{1,0:T(8,128)} %v_ref.1, f32[24,64,64]{2,1,0:T(8,128)} %t_ref.1, f32[6144,256]{1,0:T(8,128)} %z_ref.1), custom_call_target="tpu_custom_call" | custom-call | tf_op jit(solution)/shard_map/pallas_call | solution.py:305
  526.3 6.2 %copy.5 = f32[3072,512]{1,0:T(8,128)} copy(f32[3072,512]{1,0:T(8,128)} %get-tuple-element.6) | data formatting | bytes 12582912

commit v2 on v1

v2 whole, which is shorter than its diff:
```python
import jax
import jax.numpy as jnp
from jax import lax
from jax.experimental import pallas as pl
from jax.experimental.pallas import tpu as pltpu
from jax.sharding import PartitionSpec as P

FULL = lax.Precision.HIGHEST
MESH = pl.DeviceIdType.MESH
NB = 256
TR = 512


def mm(a, b):
    return lax.dot_general(a, b, (((1,), (0,)), ((), ())), precision=FULL, preferred_element_type=jnp.float32)


def mtm(a, b):
    return lax.dot_general(a, b, (((0,), (0,)), ((), ())), precision=FULL, preferred_element_type=jnp.float32)


def kernel(
    v_ref, t_ref, z_ref, out_ref, vall,
    x, vs, tb, gown, grecv, ts, ws, wr, ys, w2, y2,
    far_s, far_r, sib_s, sib_r, dia_s, dia_r, up_s, up_r, down_s, t_s, t_r, w_s, w_r, z_s, z_r, g_s, g_r, loc, ld,
):
    r = lax.axis_index("row")
    c = lax.axis_index("col")
    rows = v_ref.shape[0]
    slots = v_ref.shape[1] // NB
    tiles = rows // TR
    per_row = rows // NB
    sib = c + 1 - 2 * (c % 2)
    far = (c + 2) % 4
    other = 1 - r

    barrier = pltpu.get_barrier_semaphore()
    for dst in ((r, sib), (r, far), (other, c), (other, far)):
        pl.semaphore_signal(barrier, inc=1, device_id=dst, device_id_type=MESH)
    pl.semaphore_wait(barrier, 4)

    def first_tile(j):
        return lax.min(lax.max(j - per_row * r, 0) * NB // TR, tiles)

    def tile(k):
        return pl.ds(pl.multiple_of(k * TR, TR), TR)

    def each_tile(j, fn):
        def body(k, carry):
            fn(k)
            return carry

        lax.fori_loop(first_tile(j), tiles, body, 0)

    def own_tile(s, k):
        return v_ref.at[tile(k), pl.ds(pl.multiple_of(s * NB, NB), NB)]

    def remote(src, dst, ssem, rsem, to):
        return pltpu.make_async_remote_copy(src_ref=src, dst_ref=dst, send_sem=ssem, recv_sem=rsem, device_id=to, device_id_type=MESH)

    def own_copy(s, k, ssem, rsem, to, to_row=r):
        return remote(own_tile(s, k), vall.at[c * slots + s, tile(k)], ssem.at[s, k], rsem.at[s, k], (to_row, to))

    def got_copy(j, s, k, ssem, rsem, to):
        return remote(vall.at[j, tile(k)], vall.at[j, tile(k)], ssem.at[s, k], rsem.at[s, k], (r, to))

    def by_row0(j, k):
        upper = (j >= per_row) & (k % 3 == 2)
        lower_part = (j < per_row) & ((k == 5) | ((k == 2) & (j % 4 == 3)))
        return (j < 0) & upper & lower_part

    def direct_tile(s, fn):
        j = c * slots + s

        def body(k):
            @pl.when(jnp.logical_not((r == 1) & by_row0(j, k)))
            def _():
                fn(k)

        each_tile(j, body)

    def relay_tile(s, fn):
        j = c * slots + s

        def body(k, carry):
            @pl.when(by_row0(j, k))
            def _():
                fn(k)

            return carry

        lax.fori_loop(lax.max(j - per_row, 0) * NB // TR, tiles, body, 0)

    def up_copy(s, k):
        return own_copy(s, k, up_s, up_r, c, other)

    def down_copy(s, k):
        part = vall.at[c * slots + s, tile(k)]
        return remote(part, part, down_s.at[s, k], far_r.at[s, k], (other, far))

    def send_far(s):
        direct_tile(s, lambda k: own_copy(s, k, far_s, far_r, far).start())

    def send_up(s):
        relay_tile(s, lambda k: up_copy(s, k).start())

    def relay(s):
        def fn(k):
            up_copy(s, k).wait_recv()
            down_copy(s, k).start()

        relay_tile(s, fn)

    def loop_down(hi, n, fn):
        def body(i, carry):
            fn(hi - i)
            return carry

        lax.fori_loop(0, n, body, 0)

    zc = remote(z_ref.at[pl.ds(pl.multiple_of(other * rows, rows), rows)], x.at[:, pl.ds(pl.multiple_of(r * NB, NB), NB)], z_s, z_r, (other, c))

    @pl.when(r == 0)
    def _():
        zc.start()

    zl = pltpu.make_async_copy(z_ref.at[pl.ds(pl.multiple_of(r * rows, rows), rows)], x.at[:, pl.ds(pl.multiple_of(r * NB, NB), NB)], loc.at[0])
    zl.start()
    tl = pltpu.make_async_copy(t_ref, ts, loc.at[1])
    tl.start()

    odd = c % 2

    @pl.when((r == 1) & (c >= 2))
    def _():
        loop_down(slots - 1, slots, send_up)
        zc.start()

    @pl.when(odd == 1)
    def _():
        loop_down(slots - 1, slots, send_far)

    loop_down(slots - 1, slots, lambda s: each_tile(c * slots + s, lambda k: own_copy(s, k, sib_s, sib_r, sib).start()))

    def gram_load(s, k):
        return pltpu.make_async_copy(own_tile(s, k), vs.at[s % 2, tile(k)], ld.at[s % 2, k])

    def gram(s):
        j = c * slots + s

        @pl.when(s > 0)
        def _():
            each_tile(j - 1, lambda k: gram_load(s - 1, k).start())

        gown[s] = jnp.zeros((NB, NB), jnp.float32)

        def add(k):
            gram_load(s, k).wait()
            v_t = vs[s % 2, tile(k), :]
            gown[s] = gown[s] + mtm(v_t, v_t)

        each_tile(j, add)

    each_tile(c * slots + slots - 1, lambda k: gram_load(slots - 1, k).start())
    loop_down(slots - 1, slots, gram)
    tl.wait()

    def merge():
        quarter = range(0, NB, 128)
        for s in range(slots):
            tb[c * slots + s] = jnp.zeros((NB, NB), jnp.float32)
        t64 = [[ts[4 * s + i] for i in range(4)] for s in range(slots)]
        u64 = [[mm(t64[s][o // 64], gown[s, o : o + 64, o + 64 : o + 128]) for o in quarter] for s in range(slots)]
        n64 = [[-mm(u64[s][i], t64[s][2 * i + 1]) for i in range(2)] for s in range(slots)]
        for s in range(slots):
            j = c * slots + s
            for i, o in enumerate(quarter):
                tb[j, o : o + 64, o : o + 64] = t64[s][2 * i]
                tb[j, o + 64 : o + 128, o + 64 : o + 128] = t64[s][2 * i + 1]
                tb[j, o : o + 64, o + 64 : o + 128] = n64[s][i]
        u128 = [mm(tb[c * slots + s, 0:128, 0:128], gown[s, 0:128, 128:256]) for s in range(slots)]
        for s in range(slots):
            j = c * slots + s
            tb[j, 0:128, 128:256] = -mm(u128[s], tb[j, 128:256, 128:256])

    def t_sib(q):
        part = tb.at[pl.ds(q * slots, slots)]
        return remote(part, part, t_s.at[0], t_r.at[0], (r, sib))

    def t_chip(x_of, i, to):
        part = tb.at[pl.ds(x_of * 2 * slots, 2 * slots)]
        return remote(part, part, t_s.at[i], t_r.at[i], (r, to))

    chip = c // 2

    def factors():
        merge()
        t_sib(c).start()
        t_sib(sib).wait_recv()

        @pl.when(odd == 0)
        def _():
            t_chip(chip, 1, far).start()

    gc = remote(gown, grecv, g_s, g_r, (other, c))

    @pl.when(c < 2)
    def _():
        gc.start()

    @pl.when((r == 1) & (c < 2))
    def _():
        loop_down(slots - 1, slots, send_up)
        zc.start()

    @pl.when((c >= 2) & (r == 1))
    def _():
        factors()

    @pl.when(c == 2)
    def _():
        loop_down(slots - 1, slots, send_far)

    def t_far():
        @pl.when(odd == 0)
        def _():
            t_chip(1 - chip, 1, far).wait_recv()
            t_chip(1 - chip, 2, sib).start()

        @pl.when(odd == 1)
        def _():
            t_chip(1 - chip, 2, sib).wait_recv()

    def load(j, k):
        return pltpu.make_async_copy(vall.at[j, tile(k)], vs.at[j % 2, tile(k)], ld.at[j % 2, k])

    def arrive(j):
        q, s = j // slots, j % slots

        @pl.when(q == c)
        def _():
            each_tile(j, lambda k: pltpu.make_async_copy(own_tile(s, k), vs.at[j % 2, tile(k)], ld.at[j % 2, k]).start())

        @pl.when(q == sib)
        def _():
            def fn(k):
                got_copy(j, s, k, sib_s, sib_r, sib).wait_recv()
                load(j, k).start()

            each_tile(j, fn)

        @pl.when(q == far)
        def _():
            def fn(k):
                got_copy(j, s, k, far_s, far_r, far).wait_recv()
                got_copy(j, s, k, dia_s, dia_r, sib).start()
                load(j, k).start()

            each_tile(j, fn)

        @pl.when((q + 2) % 4 == sib)
        def _():
            def fn(k):
                got_copy(j, s, k, dia_s, dia_r, sib).wait_recv()
                load(j, k).start()

            each_tile(j, fn)

    def ahead(j):
        return (j // slots // 2 == c // 2) & (j % slots != slots - 1)

    def ready(j):
        @pl.when(jnp.logical_not(ahead(j)))
        def _():
            arrive(j)

        each_tile(j, lambda k: load(j, k).wait())

    def next_load(j):
        @pl.when((j % slots != 0) & ahead(j - 1))
        def _():
            arrive(j - 1)

    def tile_pairs(j, fn):
        lo = first_tile(j)

        @pl.when(lo % 2 == 1)
        def _():
            fn(tile(lo))

        def body(i, carry):
            fn(pl.ds(pl.multiple_of(i * 2 * TR, 2 * TR), 2 * TR))
            return carry

        lax.fori_loop((lo + 1) // 2, tiles // 2, body, 0)

    def project(j, p):
        ws[p] = jnp.zeros((NB, NB), jnp.float32)

        def add(rng):
            ws[p] = ws[p] + mtm(vs[j % 2, rng, :], x[rng, p * NB : (p + 1) * NB])

        tile_pairs(j, add)

    def update(j, p):
        def sub(rng):
            x[rng, p * NB : (p + 1) * NB] = x[rng, p * NB : (p + 1) * NB] - mm(vs[j % 2, rng, :], ys[p])

        tile_pairs(j, sub)

    zl.wait()

    @pl.when((r == 0) & (c >= 2))
    def _():
        loop_down(slots - 1, slots, relay)

    @pl.when(r == 1)
    def _():
        zc.wait()

    def lower(j):
        ready(j)
        next_load(j)
        w2[...] = jnp.zeros_like(w2)

        def add(rng):
            w2[...] = w2[...] + mtm(vs[j % 2, rng, :], x[rng, :])

        tile_pairs(j, add)
        y2[...] = mm(tb[j], w2[...])

        def sub(rng):
            x[rng, :] = x[rng, :] - mm(vs[j % 2, rng, :], y2[...])

        tile_pairs(j, sub)

        @pl.when((c == 0) & (j < 3 * slots))
        def _():
            send_far(j - 2 * slots)

    @pl.when(r == 1)
    def _():
        @pl.when(c < 2)
        def _():
            t_far()

        loop_down(4 * slots - 1, slots, lower)

    @pl.when(c < 2)
    def _():
        gc.wait()

        def add(s):
            gown[s] = gown[s] + grecv[s]

        loop_down(slots - 1, slots, add)
        factors()

    @pl.when((r == 0) & (c == 0))
    def _():
        loop_down(slots - 1, slots, send_far)

    @pl.when((r == 0) & (c < 2))
    def _():
        loop_down(slots - 1, slots, relay)

    @pl.when(r == 1)
    def _():
        loop_down(3 * slots - 1, slots, lower)

    def w_copy(j, p):
        return remote(ws.at[p], wr.at[p, j % 2], w_s.at[p, j % 2], w_r.at[p, j % 2], (other, c))

    def finish(j, p):
        w_copy(j, p).wait()
        ys[p] = mm(tb[j], ws[p] + wr[p, j % 2])
        update(j, p)

    def both(j):
        ready(j)
        project(j, 0)
        w_copy(j, 0).start()

        @pl.when(j < 2 * slots - 1)
        def _():
            finish(j + 1, 1)

        next_load(j)
        project(j, 1)
        w_copy(j, 1).start()
        finish(j, 0)

    @pl.when(r == 0)
    def _():
        zc.wait()

    @pl.when(c >= 2)
    def _():
        t_far()

    loop_down(2 * slots - 1, 2 * slots, both)
    outs = [pltpu.make_async_copy(x.at[:, pl.ds(p * NB, NB)], out_ref.at[:, pl.ds(p * NB, NB)], loc.at[p]) for p in range(2)]
    outs[0].start()
    finish(0, 1)
    outs[1].start()

    def sent(s):
        j = c * slots + s
        direct_tile(s, lambda k: own_copy(s, k, far_s, far_r, far).wait_send())

        @pl.when(r == 1)
        def _():
            relay_tile(s, lambda k: up_copy(s, k).wait_send())

        @pl.when(r == 0)
        def _():
            relay_tile(s, lambda k: down_copy(s, k).wait_send())

        each_tile(j, lambda k: own_copy(s, k, sib_s, sib_r, sib).wait_send())
        each_tile(far * slots + s, lambda k: got_copy(far * slots + s, s, k, dia_s, dia_r, sib).wait_send())

    loop_down(slots - 1, slots, sent)

    @pl.when((r == 1) | (c < 2))
    def _():
        t_sib(c).wait_send()

        @pl.when(odd == 0)
        def _():
            t_chip(chip, 1, far).wait_send()

    @pl.when(((r == 1) | (c >= 2)) & (odd == 0))
    def _():
        t_chip(1 - chip, 2, sib).wait_send()

    for o in outs:
        o.wait()


def solution(mesh):
    def local_program(v, t, z):
        rows, width = v.shape
        slots = width // NB
        f32 = jnp.float32
        any_spec = pl.BlockSpec(memory_space=pl.ANY)
        dma = pltpu.SemaphoreType.DMA
        out, _ = pl.pallas_call(
            kernel,
            out_shape=[jax.ShapeDtypeStruct((rows, 2 * NB), f32), jax.ShapeDtypeStruct((4 * slots, rows, NB), f32)],
            in_specs=[any_spec] * 3,
            out_specs=[any_spec] * 2,
            scratch_shapes=[
                pltpu.VMEM((rows, 2 * NB), f32),
                pltpu.VMEM((2, rows, NB), f32),
                pltpu.VMEM((4 * slots, NB, NB), f32),
                pltpu.VMEM((slots, NB, NB), f32),
                pltpu.VMEM((slots, NB, NB), f32),
                pltpu.VMEM(t.shape, f32),
                pltpu.VMEM((2, NB, NB), f32),
                pltpu.VMEM((2, 2, NB, NB), f32),
                pltpu.VMEM((2, NB, NB), f32),
                pltpu.VMEM((NB, 2 * NB), f32),
                pltpu.VMEM((NB, 2 * NB), f32),
                *[dma((slots, rows // TR))] * 9,
                dma((3,)), dma((3,)), dma((2, 2)), dma((2, 2)),
                dma, dma, dma, dma, dma((2,)), dma((2, rows // TR)),
            ],
            compiler_params=pltpu.CompilerParams(collective_id=0, has_side_effects=True, vmem_limit_bytes=60 * 1024 * 1024),
        )(v, t, z)
        return out

    return jax.shard_map(local_program, mesh=mesh, in_specs=(P("row", "col"), P("col", None, None), P(None, ("col", "row"))), out_specs=P("row", "col"), check_vma=False)
```

time: 533 us -> 477 us (0.89)
  Pallas kernels: 526 us -> 469 us
    pallas_call x1, Pallas kernels: 526 us -> 469 us  [local_program(): pl.pallas_call(kernel, out_shape=[jax.ShapeDtypeStruct((rows, 2 * NB), f3...]
where the time goes in v2:
time: 477 us; the launch traced here: 475 us
  Pallas kernels  469 us (98%)
  local copies, waits for them, and re-layouts  6.2 us (1%)
    pallas_call x1, Pallas kernels, local_program(): pl.pallas_call(kernel, out_shape=[jax.ShapeDtypeStruct((rows, 2 * NB), f3...  469 us

profile of v2, /device:TPU:3, one launch (start us, length us, event | category | flops | bytes accessed | tf_op | source)
XLA Modules:
  0.0 475.5 jit_solution(9207577567945548990)
XLA Ops:
  0.0 469.3 %shard_map.37 = (f32[3072,512]{1,0:T(8,128)}, f32[24,3072,256]{2,1,0:T(8,128)}) custom-call(f32[3072,1536]{1,0:T(8,128)} %v_ref.1, f32[24,64,64]{2,1,0:T(8,128)} %t_ref.1, f32[6144,256]{1,0:T(8,128)} %z_ref.1), custom_call_target="tpu_custom_call" | custom-call | tf_op jit(solution)/shard_map/pallas_call | solution.py:447
  469.3 6.2 %copy.5 = f32[3072,512]{1,0:T(8,128)} copy(f32[3072,512]{1,0:T(8,128)} %get-tuple-element.6) | data formatting | bytes 12582912

commit v3 on v2

--- a/solution.py
+++ b/solution.py
@@ -65,9 +65,9 @@
         return remote(vall.at[j, tile(k)], vall.at[j, tile(k)], ssem.at[s, k], rsem.at[s, k], (r, to))
 
     def by_row0(j, k):
-        upper = (j >= per_row) & (k % 3 == 2)
+        upper = (j >= per_row) & (j < 3 * slots) & (k % 3 == 2)
         lower_part = (j < per_row) & ((k == 5) | ((k == 2) & (j % 4 == 3)))
-        return (j < 0) & upper & lower_part
+        return upper | ((j >= slots) & (j < 2 * slots) & (k == 5))
 
     def direct_tile(s, fn):
         j = c * slots + s
@@ -131,9 +131,12 @@
 
     odd = c % 2
 
+    @pl.when((r == 1) & (c >= 1))
+    def _():
+        loop_down(slots - 1, slots, send_up)
+
     @pl.when((r == 1) & (c >= 2))
     def _():
-        loop_down(slots - 1, slots, send_up)
         zc.start()
 
     @pl.when(odd == 1)
@@ -208,9 +211,12 @@
     def _():
         gc.start()
 
+    @pl.when((r == 1) & (c == 0))
+    def _():
+        loop_down(slots - 1, slots, send_up)
+
     @pl.when((r == 1) & (c < 2))
     def _():
-        loop_down(slots - 1, slots, send_up)
         zc.start()
 
     @pl.when((c >= 2) & (r == 1))
@@ -310,7 +316,7 @@
 
     zl.wait()
 
-    @pl.when((r == 0) & (c >= 2))
+    @pl.when((r == 0) & (c >= 1))
     def _():
         loop_down(slots - 1, slots, relay)
 
@@ -358,11 +364,8 @@
 
     @pl.when((r == 0) & (c == 0))
     def _():
+        loop_down(slots - 1, slots, relay)
         loop_down(slots - 1, slots, send_far)
-
-    @pl.when((r == 0) & (c < 2))
-    def _():
-        loop_down(slots - 1, slots, relay)
 
     @pl.when(r == 1)
     def _():

time: 477 us -> 458 us (0.960)
  Pallas kernels: 469 us -> 451 us
    pallas_call x1, Pallas kernels: 469 us -> 451 us  [local_program(): pl.pallas_call(kernel, out_shape=[jax.ShapeDtypeStruct((rows, 2 * NB), f3...]
where the time goes in v3:
time: 458 us; the launch traced here: 457 us
  Pallas kernels  451 us (98%)
  local copies, waits for them, and re-layouts  6.2 us (1%)
    pallas_call x1, Pallas kernels, local_program(): pl.pallas_call(kernel, out_shape=[jax.ShapeDtypeStruct((rows, 2 * NB), f3...  451 us

profile of v3, /device:TPU:3, one launch (start us, length us, event | category | flops | bytes accessed | tf_op | source)
XLA Modules:
  0.0 457.4 jit_solution(17207830046702320713)
XLA Ops:
  0.0 451.2 %shard_map.37 = (f32[3072,512]{1,0:T(8,128)}, f32[24,3072,256]{2,1,0:T(8,128)}) custom-call(f32[3072,1536]{1,0:T(8,128)} %v_ref.1, f32[24,64,64]{2,1,0:T(8,128)} %t_ref.1, f32[6144,256]{1,0:T(8,128)} %z_ref.1), custom_call_target="tpu_custom_call" | custom-call | tf_op jit(solution)/shard_map/pallas_call | solution.py:450
  451.2 6.2 %copy.5 = f32[3072,512]{1,0:T(8,128)} copy(f32[3072,512]{1,0:T(8,128)} %get-tuple-element.6) | data formatting | bytes 12582912
